TPU v7x, 32 devices: a whole 2x2x4 slice. The times are simulated.
32 devices in a mesh: gx: 4 (over x, core), gy: 4 (over z), gz: 2 (over y).
Axes of the slice: x: 2, y: 2, z: 4, core: 2. Of those that a mesh axis runs over, the one named last changes fastest.
Arguments:
- layer_input: bfloat16 [1024, 4096], P('gz', ('gx', 'gy')), may hold values from -6 to 6
- modality: int32 [1024], P('gz'), may hold values 0 or 1
- image_spans: int32 [2, 8], replicated, may hold values from 0 to 1024, as said below
- norm_gain: float32 [2, 4096], P(None, ('gx', 'gy')), may hold values from 0.1 to 1.9
- w_qkv: bfloat16 [3, 4096, 2048], P(None, 'gz', ('gx', 'gy')), as said below
- w_out: bfloat16 [2048, 4096], P(('gx', 'gy'), 'gz'), may hold values from -0.125 to 0.125
- grad_out: bfloat16 [1024, 4096], P('gz', ('gx', 'gy')), may hold values from -6 to 6
Outputs:
- attn_out: bfloat16 [1024, 4096], P('gz', ('gx', 'gy'))
- grad_in: bfloat16 [1024, 4096], P('gz', ('gx', 'gy'))
- grad_qkv: float32 [3, 4096, 2048], P(None, 'gz', ('gx', 'gy'))
- grad_wout: float32 [2048, 4096], P(('gx', 'gy'), 'gz')
- grad_gain: float32 [2, 4096], P(None, ('gx', 'gy'))
Inputs may be any that keep to these rules, and one draw needn't show every extreme that they name: `image_spans`: row 0 holds the first position of each of 8 image spans, in increasing order, and row 1 one past its last; spans are disjoint and none is empty. `w_qkv`: entries are at most 20 * 4096 ** -0.5 in magnitude.
All inputs are finite; a program needn't handle non-finite values. No bound on the sum of `modality` on one device may be relied on, other than what follows from the above.
Results may differ from a plain program's by a relative error of at most 0.035.
The roundings to bfloat16 on the way count: a program that leaves them out, or rounds other values in their place, can miss the bound.
Values may be sent and summed in bfloat16 or wider, within the bound.
A program may use at most 128 MiB of HBM per device.

v0:
```python
import math
import jax
import jax.numpy as jnp
from jax import lax
from jax.sharding import PartitionSpec as P

epsilon = 1e-05
masked_low = -1e30


def span_index(positions, image_spans):
    inside = (positions[:, None] >= image_spans[0][None, :]) & (
        positions[:, None] < image_spans[1][None, :]
    )
    labels = jnp.arange(1, image_spans.shape[1] + 1, dtype=jnp.int32)
    return jnp.sum(jnp.where(inside, labels[None, :], 0), axis=1) - 1


def visible(query_pos, query_span, key_pos, key_span):
    causal = key_pos[None, :] <= query_pos[:, None]
    same_image = (query_span[:, None] == key_span[None, :]) & (query_span[:, None] >= 0)
    return causal | same_image


def per_device(layer_input, modality, image_spans, norm_gain, w_qkv, w_out, grad_out):
    tok_rows, local_width = layer_input.shape
    full_width = local_width * lax.axis_size(("gx", "gy"))
    head_dim = w_qkv.shape[2]
    inputs_f = layer_input.astype(jnp.float32)
    squares = lax.psum(jnp.sum(inputs_f * inputs_f, axis=1), ("gx", "gy"))
    inv_rms = lax.rsqrt(squares / full_width + epsilon)
    row_gain = jnp.where(modality[:, None] == 1, norm_gain[1][None, :], norm_gain[0][None, :])
    scaled = inputs_f * inv_rms[:, None]
    normed = (scaled * row_gain).astype(jnp.bfloat16)
    w_full = lax.all_gather(w_qkv, "gz", axis=1, tiled=True)
    wo_full = lax.all_gather(w_out, "gz", axis=1, tiled=True)
    rows_block = w_full
    projected = jnp.einsum(
        "tc,mch->mth",
        lax.all_gather(normed, ("gx", "gy"), axis=1, tiled=True),
        rows_block,
        preferred_element_type=jnp.float32,
    )
    projected = projected.astype(jnp.bfloat16)
    queries = projected[0]
    keys_values = lax.all_gather(
        jnp.concatenate([projected[1], projected[2]], axis=1), "gz", axis=0, tiled=True
    )
    key_total = keys_values.shape[0]
    query_pos = lax.axis_index("gz") * tok_rows + jnp.arange(tok_rows, dtype=jnp.int32)
    query_span = span_index(query_pos, image_spans)
    key_block = 512
    block_count = key_total // key_block
    score_scale = 1.0 / math.sqrt(head_dim)
    block_ids = jnp.arange(block_count, dtype=jnp.int32)

    def block_scores(block_idx):
        first_key = block_idx * key_block
        kv_block = lax.dynamic_slice_in_dim(keys_values, first_key, key_block, 0)
        key_pos = first_key + jnp.arange(key_block, dtype=jnp.int32)
        allowed = visible(query_pos, query_span, key_pos, span_index(key_pos, image_spans))
        scores = (
            lax.dot_general(
                queries,
                kv_block[:, :head_dim],
                (((1,), (1,)), ((), ())),
                preferred_element_type=jnp.float32,
            )
            * score_scale
        )
        return (kv_block, allowed, scores)

    def gather_stats(state, block_idx):
        maxima, summed = state
        kv_block, allowed, scores = block_scores(block_idx)
        new_maxima = jnp.maximum(maxima, jnp.max(jnp.where(allowed, scores, masked_low), axis=1))
        fresh = jnp.sum(jnp.where(allowed, jnp.exp(scores - new_maxima[:, None]), 0.0), axis=1)
        return ((new_maxima, summed * jnp.exp(maxima - new_maxima) + fresh), None)

    start_state = (
        jnp.full((tok_rows,), masked_low, jnp.float32),
        jnp.zeros((tok_rows,), jnp.float32),
    )
    (maxima, summed), unused = lax.scan(gather_stats, start_state, block_ids)
    lse = maxima + jnp.log(summed)

    def block_probs(block_idx):
        kv_block, allowed, scores = block_scores(block_idx)
        return (kv_block, jnp.where(allowed, jnp.exp(scores - lse[:, None]), 0.0))

    def attend(accum, block_idx):
        kv_block, attn_p = block_probs(block_idx)
        return (
            accum
            + jnp.dot(
                attn_p.astype(jnp.bfloat16),
                kv_block[:, head_dim:],
                preferred_element_type=jnp.float32,
            ),
            None,
        )

    attended_f, unused = lax.scan(attend, jnp.zeros((tok_rows, head_dim), jnp.float32), block_ids)
    attended = attended_f.astype(jnp.bfloat16)
    all_heads = lax.all_gather(attended, ("gx", "gy"), axis=1, tiled=True)
    out_rows = lax.all_to_all(wo_full, ("gx", "gy"), split_axis=1, concat_axis=0, tiled=True)
    head_total = out_rows.shape[0] // head_dim
    per_head = jnp.einsum(
        "thd,hdc->htc",
        all_heads.reshape(tok_rows, head_total, head_dim),
        out_rows.reshape(head_total, head_dim, local_width),
        preferred_element_type=jnp.float32,
    )
    per_head = lax.optimization_barrier(per_head.astype(jnp.bfloat16)).astype(jnp.float32)
    attn_out = jnp.sum(per_head, axis=0).astype(jnp.bfloat16)
    segment = lax.all_gather(grad_out, ("gx", "gy"), axis=1, tiled=True)
    d_accum = lax.dot_general(
        segment, wo_full, (((1,), (1,)), ((), ())), preferred_element_type=jnp.float32
    )
    partial_value = lax.dot_general(
        attended, segment, (((0,), (0,)), ((), ())), preferred_element_type=jnp.float32
    )
    d_attended = d_accum.astype(jnp.bfloat16)
    row_dots = jnp.sum(d_attended.astype(jnp.float32) * attended.astype(jnp.float32), axis=1)

    def backward_block(d_query, block_idx):
        kv_block, attn_p = block_probs(block_idx)
        d_probs = lax.dot_general(
            d_attended,
            kv_block[:, head_dim:],
            (((1,), (1,)), ((), ())),
            preferred_element_type=jnp.float32,
        )
        d_scores = (attn_p * (d_probs - row_dots[:, None]) * score_scale).astype(jnp.bfloat16)
        d_query = d_query + jnp.dot(
            d_scores, kv_block[:, :head_dim], preferred_element_type=jnp.float32
        )
        d_keys = lax.dot_general(
            d_scores, queries, (((0,), (0,)), ((), ())), preferred_element_type=jnp.float32
        )
        d_values = lax.dot_general(
            attn_p.astype(jnp.bfloat16),
            d_attended,
            (((0,), (0,)), ((), ())),
            preferred_element_type=jnp.float32,
        )
        return (d_query, jnp.concatenate([d_keys, d_values], axis=1))

    d_query_f, kv_parts = lax.scan(
        backward_block, jnp.zeros((tok_rows, head_dim), jnp.float32), block_ids
    )
    kv_grad = lax.psum_scatter(
        kv_parts.reshape(key_total, 2 * head_dim).astype(jnp.bfloat16),
        "gz",
        scatter_dimension=0,
        tiled=True,
    ).astype(jnp.float32)
    grads = jnp.stack(
        [
            d_query_f.astype(jnp.bfloat16),
            kv_grad[:, :head_dim].astype(jnp.bfloat16),
            kv_grad[:, head_dim:].astype(jnp.bfloat16),
        ]
    )
    w_grad = jnp.einsum(
        "tc,mth->mch",
        lax.all_gather(normed, ("gx", "gy"), axis=1, tiled=True),
        grads,
        preferred_element_type=jnp.float32,
    )
    grad_qkv, grad_wout = (
        lax.psum_scatter(w_grad.astype(jnp.bfloat16), "gz", scatter_dimension=1, tiled=True).astype(
            jnp.float32
        ),
        lax.psum_scatter(
            partial_value.astype(jnp.bfloat16), "gz", scatter_dimension=1, tiled=True
        ).astype(jnp.float32),
    )
    rows_block = w_full
    grad_normed = (
        lax.psum_scatter(
            jnp.einsum("mch,mth->ct", rows_block, grads, preferred_element_type=jnp.float32).astype(
                jnp.bfloat16
            ),
            ("gx", "gy"),
            scatter_dimension=0,
            tiled=True,
        )
        .astype(jnp.float32)
        .T
    )
    upstream = grad_normed * row_gain
    norm_dots = lax.psum(jnp.sum(upstream * scaled, axis=1), ("gx", "gy"))
    grad_in = (inv_rms[:, None] * (upstream - scaled * (norm_dots / full_width)[:, None])).astype(
        jnp.bfloat16
    )
    onehot = (modality[:, None] == jnp.arange(2, dtype=jnp.int32)[None, :]).astype(jnp.float32)
    local_gain = jnp.dot(onehot.T, grad_normed * scaled, precision=lax.Precision.HIGHEST)
    grad_gain = lax.psum(local_gain, "gz")
    return (attn_out, grad_in, grad_qkv, grad_wout, grad_gain)


def solution(mesh):
    in_specs = (
        P("gz", ("gx", "gy")),
        P("gz"),
        P(),
        P(None, ("gx", "gy")),
        P(None, "gz", ("gx", "gy")),
        P(("gx", "gy"), "gz"),
        P("gz", ("gx", "gy")),
    )
    out_specs = (
        P("gz", ("gx", "gy")),
        P("gz", ("gx", "gy")),
        P(None, "gz", ("gx", "gy")),
        P(("gx", "gy"), "gz"),
        P(None, ("gx", "gy")),
    )
    return jax.shard_map(
        per_device, mesh=mesh, in_specs=in_specs, out_specs=out_specs, check_vma=False
    )
```

profile of v0, /device:TPU:0, one launch (start us, length us, event | category | flops | bytes accessed | tf_op | source)
XLA Modules:
  0.0 420.7 jit_solution(4267195177550142330)
XLA Ops:
  7.3 2.7 copy.44
  10.2 35.2 %psum.21 = f32[512]{0:T(512)S(1)} all-reduce(f32[512]{0:T(512)S(1)} %fusion.65), channel_id=1, replica_groups=mesh['gx'=4,'gy'=4,'gz'=2] {'gx','gy'}, use_global_device_ids=true, to_apply=%region_1.0 | all-reduce | flops 512 | bytes 4096 | tf_op jit(solution)/shard_map/psum | solution.py:30
  45.4 0.9 fusion.66
  46.4 1.0 copy.50
  47.5 0.5 all-gather.14.cloned.1.call-update
  48.3 9.5 %all-gather.8.cloned.1.call-done = bf16[3,4096,128]{1,2,0:T(8,128)(2,1)} async-done(((bf16[3,2048,128]{1,2,0:T(8,128)(2,1)}), bf16[3,4096,128]{1,2,0:T(8,128)(2,1)}) %all-gather.8.cloned.1.call-update) | async-done | bytes 3145744 | tf_op jit(solution)/shard_map/all_gather | solution.py:35
  57.8 55.2 %all-gather.6.cloned.1.call-done = bf16[512,4096]{1,0:T(8,128)(2,1)} async-done(((bf16[512,256]{1,0:T(8,128)(2,1)}), bf16[512,4096]{1,0:T(8,128)(2,1)}) %all-gather.6.cloned.1.call-update) | async-done | bytes 4194320 | tf_op jit(solution)/shard_map/all_gather | solution.py:40
  113.0 5.0 %fusion.75 = f32[512,384]{0,1:S(1)} fusion(bf16[512,4096]{1,0:T(8,128)(2,1)} %all-gather.6.cloned.1.call-done, bf16[4096,384]{0,1:T(8,128)(2,1)} %bitcast.156), kind=kOutput, calls=%fused_computation.134 | convolution fusion | flops 1610612736 | bytes 8126464
  118.1 13.9 %all_gather.21 = bf16[1024,256]{0,1:T(8,128)(2,1)S(1)} all-gather(bf16[512,256]{0,1:T(8,128)(2,1)S(1)} %pad_maximum_fusion.1), channel_id=1, replica_groups=mesh['gx'=4,'gy'=4,'gz'=2] {'gz'}, dimensions={0}, use_global_device_ids=true | all-gather | bytes 786432 | tf_op jit(solution)/shard_map/all_gather | solution.py:46
  132.4 4.8 %while.43 = (s32[]{:T(128)}, f32[512]{0:T(512)S(1)}, f32[512]{0:T(512)S(1)}, s32[2]{0:T(128)S(1)}, s32[512]{0:T(512)S(1)}, /*index=5*/s32[2,8]{1,0:T(2,128)S(1)}...) while((s32[]{:T(128)}, f32[512]{0:T(512)S(1)}, ...), condition=%wide.region_7.8_spmd.clone, body=%wide.region_3.7_spmd.clone.sunk | while | flops 70803472 | bytes 2418638 | solution.py:84
  132.4 0.6 dynamic_slice.46
  134.8 0.6 dynamic_slice.46
  137.2 0.6 log_add_fusion
  137.7 5.9 %while.44 = (s32[]{:T(128)}, f32[512,128]{1,0:T(8,128)S(1)}, s32[2]{0:T(128)S(1)}, s32[512]{0:T(512)S(1)}, s32[2,8]{1,0:T(2,128)S(1)}, /*index=5*/bf16[1024,256]...) while((s32[]{:T(128)}, f32[512,128]{1,0:T(8,128)S(1)}, ...), condition=%wide.region_10.11_spmd.clone, body=%wide.region_8.10_spmd.clone.sunk | while | flops 136467984 | bytes 945628 | solution.py:103
  137.7 0.6 dynamic_slice.47
  139.1 1.5 fusion.118
  140.7 0.6 dynamic_slice.47
  142.1 1.5 fusion.118
  143.8 47.6 %all-gather.14.cloned.1.call-done = bf16[512,4096]{1,0:T(8,128)(2,1)} async-done(((bf16[512,256]{1,0:T(8,128)(2,1)}), bf16[512,4096]{1,0:T(8,128)(2,1)}) %all-gather.14.cloned.1.call-update) | async-done | bytes 4194320 | tf_op jit(solution)/shard_map/all_gather | solution.py:116
  191.3 4.0 multiply_reduce_fusion
  196.0 9.3 %while.45 = (s32[]{:T(128)}, f32[512,128]{1,0:T(8,128)S(1)}, bf16[2,512,256]{1,2,0:T(8,128)(2,1)S(1)}, s32[2]{0:T(128)}, s32[512]{0:T(512)S(1)}, /*index=5*/s32[...) while((s32[]{:T(128)}, f32[512,128]{1,0:T(8,128)S(1)}, ...), condition=%wide.region_15.16_spmd.clone, body=%wide.region_13.15_spmd.clone.sunk | while | flops 339367424 | bytes 6974985 | solution.py:149
  196.0 1.2 dynamic_slice.48
  198.0 1.2 fusion.129
  200.6 1.2 dynamic_slice.48
  202.7 1.2 fusion.129
  205.3 1.0 copy.56
  206.4 3.9 convolution_convert_fusion.1
  210.3 0.7 all-gather.10.cloned.1.call-update
  211.1 8.2 %reduce-scatter.5.cloned.1.call-done = bf16[512,256]{1,0:T(8,128)(2,1)} async-done(((bf16[1024,256]{1,0:T(8,128)(2,1)}), bf16[512,256]{1,0:T(8,128)(2,1)}) %reduce-scatter.5.cloned.1.call-update) | async-done | bytes 262160 | tf_op jit(solution)/shard_map/reduce_scatter | solution.py:152
  219.2 1.0 slice_bitcast_fusion.7
  220.2 5.8 %fusion.52 = bf16[4096,512]{0,1:T(8,128)(2,1)} fusion(bf16[3,4096,128]{1,2,0:T(8,128)(2,1)} %all-gather.8.cloned.1.call-done, bf16[1,512,128]{2,1,0:T(8,128)(2,1)S(1)} %get-tuple-element.678, bf16[1,512,128]{2,1,0:T(8,128)(2,1)S(1)} %get-tuple-element.677, bf16[1,512,128]{2,1,0:T(8,128)(2,1)S(1)} %convert_bitcast_fusion.1), kind=kOutput, calls=%fused_computation.84 | convolution fusion | flops 1613103104 | bytes 7733248 | tf_op jit(solution)/shard_map/mch,mth->ct/dot_general | solution.py:182
  226.3 6.1 %fusion.53 = bf16[3,4096,128]{1,2,0:T(8,128)(2,1)} fusion(bf16[512,4096]{1,0:T(8,128)(2,1)} %all-gather.6.cloned.1.call-done, bf16[1,512,128]{2,1,0:T(8,128)(2,1)S(1)} %get-tuple-element.678, bf16[1,512,128]{2,1,0:T(8,128)(2,1)S(1)} %get-tuple-element.677, bf16[1,512,128]{2,1,0:T(8,128)(2,1)S(1)} %convert_bitcast_fusion.1), kind=kOutput, calls=%fused_computation.85 | convolution fusion | flops 1612578816 | bytes 7733248 | tf_op jit(solution)/shard_map/tc,mth->mch/dot_general | solution.py:165
  232.4 1.3 copy.51
  233.8 5.5 %all-to-all-start = ((bf16[128,16,256]{2,0,1:T(8,128)(2,1)}), bf16[128,16,256]{2,0,1:T(8,128)(2,1)S(1)}, u32[]{:S(2)}, u32[]{:S(2)}) async-start(bf16[128,16,256]{2,0,1:T(8,128)(2,1)} %copy.51), calls=%async_computation | async-start | bytes 2097152 | tf_op jit(solution)/shard_map/all_to_all | solution.py:106
  239.3 3.1 reduce-scatter.11.cloned.1.call-done
  242.4 2.1 convert_element_type.104
  244.5 25.8 %all-to-all-done = bf16[128,16,256]{2,0,1:T(8,128)(2,1)S(1)} async-done(((bf16[128,16,256]{2,0,1:T(8,128)(2,1)}), bf16[128,16,256]{2,0,1:T(8,128)(2,1)S(1)}, u32[]{:S(2)}, u32[]{:S(2)}) %all-to-all-start) | async-done | bytes 1048608 | tf_op jit(solution)/shard_map/all_to_all | solution.py:106
  270.3 19.1 %all-gather.10.cloned.1.call-done = bf16[512,2048]{0,1:T(8,128)(2,1)} async-done(((bf16[512,128]{0,1:T(8,128)(2,1)}), bf16[512,2048]{0,1:T(8,128)(2,1)}) %all-gather.10.cloned.1.call-update) | async-done | bytes 2097168 | tf_op jit(solution)/shard_map/all_gather | solution.py:105
  289.4 4.8 %convolution_convert_fusion.2 = bf16[16,512,256]{2,1,0:T(8,128)(2,1)} fusion(bf16[512,16,128]{0,2,1:T(8,128)(2,1)} %bitcast.147, bf16[128,16,256]{2,0,1:T(8,128)(2,1)S(1)} %all-to-all-done), kind=kOutput, calls=%fused_computation.88 | convolution fusion | flops 538968064 | bytes 7340032 | tf_op jit(solution)/shard_map/thd,hdc->htc/dot_general | solution.py:108
  294.2 3.5 reduce_sum.98
  297.8 67.0 %reduce-scatter.7.cloned.1.call-done = bf16[256,512]{0,1:T(8,128)(2,1)} async-done(((bf16[4096,512]{0,1:T(8,128)(2,1)}), bf16[256,512]{0,1:T(8,128)(2,1)}) %reduce-scatter.7.cloned.1.call-update) | async-done | bytes 262160 | tf_op jit(solution)/shard_map/reduce_scatter | solution.py:181
  364.8 1.3 fusion.59
  366.1 30.5 %psum.22 = f32[512]{0:T(512)S(1)} all-reduce(f32[512]{0:T(512)S(1)} %fusion.59), channel_id=1, replica_groups=mesh['gx'=4,'gy'=4,'gz'=2] {'gx','gy'}, use_global_device_ids=true, to_apply=%region_19.20 | all-reduce | flops 512 | bytes 4096 | tf_op jit(solution)/shard_map/psum | solution.py:193
  396.6 1.5 fusion.63
  398.1 5.7 %psum.23 = f32[2,256]{1,0:T(2,128)} all-reduce(f32[2,256]{1,0:T(2,128)S(1)} %fusion.63), channel_id=1, replica_groups=mesh['gx'=4,'gy'=4,'gz'=2] {'gz'}, use_global_device_ids=true, to_apply=%region_22.23 | all-reduce | flops 512 | bytes 4096 | tf_op jit(solution)/shard_map/psum | solution.py:199
  403.8 6.4 %reduce-scatter.9.cloned.1.call-done = bf16[3,2048,128]{1,2,0:T(8,128)(2,1)} async-done(((bf16[3,4096,128]{1,2,0:T(8,128)(2,1)}), bf16[3,2048,128]{1,2,0:T(8,128)(2,1)}) %reduce-scatter.9.cloned.1.call-update) | async-done | bytes 1572880 | tf_op jit(solution)/shard_map/reduce_scatter | solution.py:172
  410.2 3.1 copy.59
  413.2 1.0 fusion.62
  (129 shorter events, 7.5 us)
Async XLA Ops:
  7.2 2.8 copy-start
  7.2 38.2 %copy-start.12 = (s32[512]{0:T(512)S(1)}, s32[512]{0:T(512)}, u32[]{:S(2)}) copy-start(s32[512]{0:T(512)} %param.14) | copy-start | bytes 6148
  7.2 38.2 %copy-start.14 = (f32[2,256]{1,0:T(2,128)S(1)}, f32[2,256]{1,0:T(2,128)}, u32[]{:S(2)}) copy-start(f32[2,256]{1,0:T(2,128)} %param.16) | copy-start | bytes 6148
  7.2 39.2 %copy-start.4 = (bf16[128,2048]{1,0:T(8,128)(2,1)S(1)}, bf16[128,2048]{1,0:T(8,128)(2,1)}, u32[]{:S(2)}) copy-start(bf16[128,2048]{1,0:T(8,128)(2,1)} %param.18) | copy-start | bytes 1572868
  7.2 41.0 %copy-start.5 = (s32[2,8]{1,0:T(2,128)S(1)}, s32[2,8]{1,0:T(2,128)}, u32[]{:S(2)}) copy-start(s32[2,8]{1,0:T(2,128)} %param.15) | copy-start | bytes 196
  7.2 50.6 %all-gather.8.cloned.1.call-start = ((), (), s32[]{:S(2)}) async-start(), calls=%async_computation.6 | async-start | bytes 4718592 | tf_op jit(solution)/shard_map/all_gather | solution.py:35
  10.0 103.0 %all-gather.6.cloned.1.call-start = ((), (), s32[]{:S(2)}) async-start(), calls=%async_computation.5 | async-start | bytes 4456448 | tf_op jit(solution)/shard_map/all_gather | solution.py:40
  45.4 2.8 copy-start.10
  45.4 2.7 copy-start.8
  45.4 72.6 %copy-start.6 = (f32[1,256]{1,0:T(1,128)}, f32[1,256]{1,0:T(1,128)S(1)}, u32[]{:S(2)}) copy-start(f32[1,256]{1,0:T(1,128)S(1)} %get-tuple-element.679) | copy-start | bytes 3076
  46.3 97.4 %all-gather.12.cloned.1.call-start = ((), (), s32[]{:S(2)}) async-start(), calls=%async_computation.8 | async-start | bytes 1572864 | tf_op jit(solution)/shard_map/all_gather | solution.py:36
  47.4 143.9 %all-gather.14.cloned.1.call-start = ((), (), s32[]{:S(2)}) async-start(), calls=%async_computation.9 | async-start | bytes 4456448 | tf_op jit(solution)/shard_map/all_gather | solution.py:116
  48.0 171.2 %reduce-scatter.5.cloned.1.call-start = ((), (), s32[]{:S(2)}) async-start(), calls=%async_computation.10 | async-start | bytes 786432 | tf_op jit(solution)/shard_map/reduce_scatter | solution.py:152
  143.7 62.6 %copy-start.2 = (bf16[512,128]{0,1:T(8,128)(2,1)}, bf16[512,128]{0,1:T(8,128)(2,1)S(1)}, u32[]{:S(2)}) copy-start(bf16[512,128]{0,1:T(8,128)(2,1)S(1)} %copy.49) | copy-start | bytes 393220
  206.3 36.1 %reduce-scatter.11.cloned.1.call-start = ((), (), s32[]{:S(2)}) async-start(), calls=%async_computation.13 | async-start | bytes 1572864 | tf_op jit(solution)/shard_map/reduce_scatter | solution.py:175
  210.3 79.1 %all-gather.10.cloned.1.call-start = ((), (), s32[]{:S(2)}) async-start(), calls=%async_computation.7 | async-start | bytes 2228224 | tf_op jit(solution)/shard_map/all_gather | solution.py:105
  211.0 153.8 %reduce-scatter.7.cloned.1.call-start = ((), (), s32[]{:S(2)}) async-start(), calls=%async_computation.11 | async-start | bytes 4456448 | tf_op jit(solution)/shard_map/reduce_scatter | solution.py:181
  226.1 6.4 %copy-start.1 = (bf16[128,4096]{0,1:T(8,128)(2,1)S(1)}, bf16[128,4096]{0,1:T(8,128)(2,1)}, u32[]{:S(2)}) copy-start(bf16[128,4096]{0,1:T(8,128)(2,1)} %all-gather.12.cloned.1.call-done) | copy-start | bytes 3145732
  226.1 184.1 %reduce-scatter.9.cloned.1.call-start = ((), (), s32[]{:S(2)}) async-start(), calls=%async_computation.12 | async-start | bytes 4718592 | tf_op jit(solution)/shard_map/reduce_scatter | solution.py:172
  233.8 36.5 %all-to-all-start = ((bf16[128,16,256]{2,0,1:T(8,128)(2,1)}), bf16[128,16,256]{2,0,1:T(8,128)(2,1)S(1)}, u32[]{:S(2)}, u32[]{:S(2)}) async-start(bf16[128,16,256]{2,0,1:T(8,128)(2,1)} %copy.51), calls=%async_computation | async-start | bytes 2097152 | tf_op jit(solution)/shard_map/all_to_all | solution.py:106
  289.4 75.4 %copy-start.7 = (f32[1,256]{1,0:T(1,128)S(1)}, f32[1,256]{1,0:T(1,128)}, u32[]{:S(2)}) copy-start(f32[1,256]{1,0:T(1,128)} %copy-done.6) | copy-start | bytes 3076
  289.4 75.4 %copy-start.9 = (f32[1,256]{1,0:T(1,128)S(1)}, f32[1,256]{1,0:T(1,128)}, u32[]{:S(2)}) copy-start(f32[1,256]{1,0:T(1,128)} %copy-done.8) | copy-start | bytes 3076
  289.4 75.4 %copy-start.11 = (pred[512]{0:T(512)(128)(4,1)S(1)}, pred[512]{0:T(512)(128)(4,1)}, u32[]{:S(2)}) copy-start(pred[512]{0:T(512)(128)(4,1)} %copy-done.10) | copy-start | bytes 1540
  294.2 102.4 %copy-start.13 = (s32[512]{0:T(512)S(1)}, s32[512]{0:T(512)}, u32[]{:S(2)}) copy-start(s32[512]{0:T(512)} %param.14) | copy-start | bytes 6148
  364.8 48.5 %copy-start.3 = (bf16[256,512]{0,1:T(8,128)(2,1)S(1)}, bf16[256,512]{0,1:T(8,128)(2,1)}, u32[]{:S(2)}) copy-start(bf16[256,512]{0,1:T(8,128)(2,1)} %reduce-scatter.7.cloned.1.call-done) | copy-start | bytes 786436
Sparse Core Ops, SparseCore 0:
  10.1 47.6 all-gather.7
  60.5 52.4 all-gather.5
  115.1 23.5 all-gather.11
  140.6 50.6 all-gather.13
  206.4 12.7 reduce-scatter.4
  221.9 20.3 reduce-scatter.10
  245.1 44.2 all-gather.9
  293.3 71.4 reduce-scatter.6
  367.6 42.5 reduce-scatter.8
where the time goes:
time: 421 us
  waiting for transfers between devices  243 us (58%)
  blocking collectives  85.3 us (20%)
  matrix products  40.2 us (10%)
  local copies, waits for them, and re-layouts  16.1 us (4%)
  between operations  14.2 us (3%)
  other arithmetic  11.5 us (3%)
  starting transfers between devices  6.02 us (1%)
  loops' own time  4.31 us (1%)
    reduce_scatter x1, waiting for transfers between devices, per_device(): lax.psum_scatter(jnp.einsum('mch,mth->ct', rows_block, grads, preferred_e...  67 us
    all_gather x1, waiting for transfers between devices, per_device(): lax.all_gather(normed, ('gx', 'gy'), axis=1, tiled=True)  55.2 us
    all_gather x1, waiting for transfers between devices, per_device(): segment = lax.all_gather(grad_out, ('gx', 'gy'), axis=1, tiled=True)  47.6 us
    psum x1, blocking collectives, per_device(): squares = lax.psum(jnp.sum(inputs_f * inputs_f, axis=1), ('gx', 'gy'))  35.2 us
    psum x1, blocking collectives, per_device(): norm_dots = lax.psum(jnp.sum(upstream * scaled, axis=1), ('gx', 'gy'))  30.5 us
    all_to_all x1, waiting for transfers between devices, per_device(): lax.all_to_all(wo_full, ('gx', 'gy'), split_axis=1, concat_axis=0, tiled=...  25.8 us
    all_gather x1, waiting for transfers between devices, per_device(): all_heads = lax.all_gather(attended, ('gx', 'gy'), axis=1, tiled=True)  19.1 us
    all_gather x1, blocking collectives, per_device(): lax.all_gather(jnp.concatenate([projected[1], projected[2]], axis=1), 'gz...  13.9 us
  transfers between devices with their start and end apart: 10, of which 9 were waited for; matrix products, arithmetic and copies ran while one was open for 11% of the time, Pallas kernels for 0%

commit v1 on v0

--- a/solution.py
+++ b/solution.py
@@ -190,7 +190,7 @@
         .T
     )
     upstream = grad_normed * row_gain
-    norm_dots = lax.psum(jnp.sum(upstream * scaled, axis=1), ("gx", "gy"))
+    norm_dots = lax.psum(lax.psum(jnp.sum(upstream * scaled, axis=1), "gx"), "gy")
     grad_in = (inv_rms[:, None] * (upstream - scaled * (norm_dots / full_width)[:, None])).astype(
         jnp.bfloat16
     )

time: 421 us -> 422 us (level)
  blocking collectives: 85.3 us -> 71.1 us
  waiting for transfers between devices: 243 us -> 257 us
    psum x1 -> x2, blocking collectives: 30.5 us -> 16.3 us  [the longest x1 10.5 us: per_device(): lax.psum(lax.psum(jnp.sum(upstream * scaled, axis=1), 'gx'), 'gy')]
    reduce_scatter x1, waiting for transfers between devices: 6.36 us -> 20.6 us  [per_device(): lax.psum_scatter(w_grad.astype(jnp.bfloat16), 'gz', scatter_dimension=1,...]
where the time goes in v1:
time: 422 us; the launch traced here: 421 us
  waiting for transfers between devices  257 us (61%)
  blocking collectives  71.1 us (17%)
  matrix products  40.1 us (10%)
  local copies, waits for them, and re-layouts  16.1 us (4%)
  between operations  14.2 us (3%)
  other arithmetic  11.5 us (3%)
  starting transfers between devices  6.02 us (1%)
  loops' own time  4.31 us (1%)
    reduce_scatter x1, waiting for transfers between devices, per_device(): lax.psum_scatter(jnp.einsum('mch,mth->ct', rows_block, grads, preferred_e...  67 us
    all_gather x1, waiting for transfers between devices, per_device(): lax.all_gather(normed, ('gx', 'gy'), axis=1, tiled=True)  55.2 us
    all_gather x1, waiting for transfers between devices, per_device(): segment = lax.all_gather(grad_out, ('gx', 'gy'), axis=1, tiled=True)  47.6 us
    psum x1, blocking collectives, per_device(): squares = lax.psum(jnp.sum(inputs_f * inputs_f, axis=1), ('gx', 'gy'))  35.2 us
    all_to_all x1, waiting for transfers between devices, per_device(): lax.all_to_all(wo_full, ('gx', 'gy'), split_axis=1, concat_axis=0, tiled=...  25.8 us
    reduce_scatter x1, waiting for transfers between devices, per_device(): lax.psum_scatter(w_grad.astype(jnp.bfloat16), 'gz', scatter_dimension=1,...  20.6 us
    all_gather x1, waiting for transfers between devices, per_device(): all_heads = lax.all_gather(attended, ('gx', 'gy'), axis=1, tiled=True)  19.1 us
    all_gather x1, blocking collectives, per_device(): lax.all_gather(jnp.concatenate([projected[1], projected[2]], axis=1), 'gz...  13.9 us
  transfers between devices with their start and end apart: 10, of which 9 were waited for; matrix products, arithmetic and copies ran while one was open for 11% of the time, Pallas kernels for 0%

profile of v1, /device:TPU:0, one launch (start us, length us, event | category | flops | bytes accessed | tf_op | source)
XLA Modules:
  0.0 420.7 jit_solution(16494984096274325145)
XLA Ops:
  7.3 2.7 copy.44
  10.2 35.2 %psum.28 = f32[512]{0:T(512)S(1)} all-reduce(f32[512]{0:T(512)S(1)} %fusion.65), channel_id=1, replica_groups=mesh['gx'=4,'gy'=4,'gz'=2] {'gx','gy'}, use_global_device_ids=true, to_apply=%region_1.0 | all-reduce | flops 512 | bytes 4096 | tf_op jit(solution)/shard_map/psum | solution.py:30
  45.4 0.9 fusion.66
  46.4 1.0 copy.50
  48.3 9.6 %all-gather.8.cloned.1.call-done = bf16[3,4096,128]{1,2,0:T(8,128)(2,1)} async-done(((bf16[3,2048,128]{1,2,0:T(8,128)(2,1)}), bf16[3,4096,128]{1,2,0:T(8,128)(2,1)}) %all-gather.8.cloned.1.call-update) | async-done | bytes 3145744 | tf_op jit(solution)/shard_map/all_gather | solution.py:35
  57.8 55.2 %all-gather.6.cloned.1.call-done = bf16[512,4096]{1,0:T(8,128)(2,1)} async-done(((bf16[512,256]{1,0:T(8,128)(2,1)}), bf16[512,4096]{1,0:T(8,128)(2,1)}) %all-gather.6.cloned.1.call-update) | async-done | bytes 4194320 | tf_op jit(solution)/shard_map/all_gather | solution.py:40
  113.0 5.0 %fusion.75 = f32[512,384]{0,1:S(1)} fusion(bf16[512,4096]{1,0:T(8,128)(2,1)} %all-gather.6.cloned.1.call-done, bf16[4096,384]{0,1:T(8,128)(2,1)} %bitcast.156), kind=kOutput, calls=%fused_computation.134 | convolution fusion | flops 1610612736 | bytes 8126464
  118.1 13.9 %all_gather.21 = bf16[1024,256]{0,1:T(8,128)(2,1)S(1)} all-gather(bf16[512,256]{0,1:T(8,128)(2,1)S(1)} %pad_maximum_fusion.1), channel_id=1, replica_groups=mesh['gx'=4,'gy'=4,'gz'=2] {'gz'}, dimensions={0}, use_global_device_ids=true | all-gather | bytes 786432 | tf_op jit(solution)/shard_map/all_gather | solution.py:46
  132.4 4.8 %while.43 = (s32[]{:T(128)}, f32[512]{0:T(512)S(1)}, f32[512]{0:T(512)S(1)}, s32[2]{0:T(128)S(1)}, s32[512]{0:T(512)S(1)}, /*index=5*/s32[2,8]{1,0:T(2,128)S(1)}...) while((s32[]{:T(128)}, f32[512]{0:T(512)S(1)}, ...), condition=%wide.region_7.8_spmd.clone, body=%wide.region_3.7_spmd.clone.sunk | while | flops 70803472 | bytes 2418638 | solution.py:84
  132.4 0.6 dynamic_slice.46
  134.8 0.6 dynamic_slice.46
  137.2 0.6 log_add_fusion
  137.8 5.9 %while.44 = (s32[]{:T(128)}, f32[512,128]{1,0:T(8,128)S(1)}, s32[2]{0:T(128)S(1)}, s32[512]{0:T(512)S(1)}, s32[2,8]{1,0:T(2,128)S(1)}, /*index=5*/bf16[1024,256]...) while((s32[]{:T(128)}, f32[512,128]{1,0:T(8,128)S(1)}, ...), condition=%wide.region_10.11_spmd.clone, body=%wide.region_8.10_spmd.clone.sunk | while | flops 136467984 | bytes 945628 | solution.py:103
  137.8 0.6 dynamic_slice.47
  139.1 1.5 fusion.118
  140.7 0.6 dynamic_slice.47
  142.1 1.5 fusion.118
  143.8 47.6 %all-gather.14.cloned.1.call-done = bf16[512,4096]{1,0:T(8,128)(2,1)} async-done(((bf16[512,256]{1,0:T(8,128)(2,1)}), bf16[512,4096]{1,0:T(8,128)(2,1)}) %all-gather.14.cloned.1.call-update) | async-done | bytes 4194320 | tf_op jit(solution)/shard_map/all_gather | solution.py:116
  191.3 4.0 multiply_reduce_fusion
  196.0 9.3 %while.45 = (s32[]{:T(128)}, f32[512,128]{1,0:T(8,128)S(1)}, bf16[2,512,256]{1,2,0:T(8,128)(2,1)S(1)}, s32[2]{0:T(128)}, s32[512]{0:T(512)S(1)}, /*index=5*/s32[...) while((s32[]{:T(128)}, f32[512,128]{1,0:T(8,128)S(1)}, ...), condition=%wide.region_15.16_spmd.clone, body=%wide.region_13.15_spmd.clone.sunk | while | flops 339367424 | bytes 6974985 | solution.py:149
  196.0 1.2 dynamic_slice.48
  198.0 1.2 fusion.129
  200.6 1.2 dynamic_slice.48
  202.7 1.2 fusion.129
  205.3 1.0 copy.56
  206.4 3.9 convolution_convert_fusion.1
  210.3 0.7 all-gather.10.cloned.1.call-update
  211.1 8.2 %reduce-scatter.5.cloned.1.call-done = bf16[512,256]{1,0:T(8,128)(2,1)} async-done(((bf16[1024,256]{1,0:T(8,128)(2,1)}), bf16[512,256]{1,0:T(8,128)(2,1)}) %reduce-scatter.5.cloned.1.call-update) | async-done | bytes 262160 | tf_op jit(solution)/shard_map/reduce_scatter | solution.py:152
  219.3 1.0 slice_bitcast_fusion.7
  220.2 5.8 %fusion.52 = bf16[4096,512]{0,1:T(8,128)(2,1)} fusion(bf16[3,4096,128]{1,2,0:T(8,128)(2,1)} %all-gather.8.cloned.1.call-done, bf16[1,512,128]{2,1,0:T(8,128)(2,1)S(1)} %get-tuple-element.678, bf16[1,512,128]{2,1,0:T(8,128)(2,1)S(1)} %get-tuple-element.677, bf16[1,512,128]{2,1,0:T(8,128)(2,1)S(1)} %convert_bitcast_fusion.1), kind=kOutput, calls=%fused_computation.84 | convolution fusion | flops 1613103104 | bytes 7733248 | tf_op jit(solution)/shard_map/mch,mth->ct/dot_general | solution.py:182
  226.3 6.1 %fusion.53 = bf16[3,4096,128]{1,2,0:T(8,128)(2,1)} fusion(bf16[512,4096]{1,0:T(8,128)(2,1)} %all-gather.6.cloned.1.call-done, bf16[1,512,128]{2,1,0:T(8,128)(2,1)S(1)} %get-tuple-element.678, bf16[1,512,128]{2,1,0:T(8,128)(2,1)S(1)} %get-tuple-element.677, bf16[1,512,128]{2,1,0:T(8,128)(2,1)S(1)} %convert_bitcast_fusion.1), kind=kOutput, calls=%fused_computation.85 | convolution fusion | flops 1612578816 | bytes 7733248 | tf_op jit(solution)/shard_map/tc,mth->mch/dot_general | solution.py:165
  232.4 1.3 copy.51
  233.8 5.5 %all-to-all-start = ((bf16[128,16,256]{2,0,1:T(8,128)(2,1)}), bf16[128,16,256]{2,0,1:T(8,128)(2,1)S(1)}, u32[]{:S(2)}, u32[]{:S(2)}) async-start(bf16[128,16,256]{2,0,1:T(8,128)(2,1)} %copy.51), calls=%async_computation | async-start | bytes 2097152 | tf_op jit(solution)/shard_map/all_to_all | solution.py:106
  239.3 3.1 reduce-scatter.11.cloned.1.call-done
  242.4 2.1 convert_element_type.104
  244.5 25.8 %all-to-all-done = bf16[128,16,256]{2,0,1:T(8,128)(2,1)S(1)} async-done(((bf16[128,16,256]{2,0,1:T(8,128)(2,1)}), bf16[128,16,256]{2,0,1:T(8,128)(2,1)S(1)}, u32[]{:S(2)}, u32[]{:S(2)}) %all-to-all-start) | async-done | bytes 1048608 | tf_op jit(solution)/shard_map/all_to_all | solution.py:106
  270.3 19.1 %all-gather.10.cloned.1.call-done = bf16[512,2048]{0,1:T(8,128)(2,1)} async-done(((bf16[512,128]{0,1:T(8,128)(2,1)}), bf16[512,2048]{0,1:T(8,128)(2,1)}) %all-gather.10.cloned.1.call-update) | async-done | bytes 2097168 | tf_op jit(solution)/shard_map/all_gather | solution.py:105
  289.4 4.8 %convolution_convert_fusion.2 = bf16[16,512,256]{2,1,0:T(8,128)(2,1)} fusion(bf16[512,16,128]{0,2,1:T(8,128)(2,1)} %bitcast.147, bf16[128,16,256]{2,0,1:T(8,128)(2,1)S(1)} %all-to-all-done), kind=kOutput, calls=%fused_computation.88 | convolution fusion | flops 538968064 | bytes 7340032 | tf_op jit(solution)/shard_map/thd,hdc->htc/dot_general | solution.py:108
  294.2 3.5 reduce_sum.98
  297.8 67.0 %reduce-scatter.7.cloned.1.call-done = bf16[256,512]{0,1:T(8,128)(2,1)} async-done(((bf16[4096,512]{0,1:T(8,128)(2,1)}), bf16[256,512]{0,1:T(8,128)(2,1)}) %reduce-scatter.7.cloned.1.call-update) | async-done | bytes 262160 | tf_op jit(solution)/shard_map/reduce_scatter | solution.py:181
  364.8 1.3 fusion.59
  366.1 5.9 %psum.29 = f32[512]{0:T(512)S(1)} all-reduce(f32[512]{0:T(512)S(1)} %fusion.59), channel_id=1, replica_groups=mesh['gx'=4,'gy'=4,'gz'=2] {'gx'}, use_global_device_ids=true, to_apply=%region_19.20 | all-reduce | flops 512 | bytes 4096 | tf_op jit(solution)/shard_map/psum | solution.py:193
  372.0 10.5 %psum.30 = f32[512]{0:T(512)S(1)} all-reduce(f32[512]{0:T(512)S(1)} %psum.29), channel_id=1, replica_groups=mesh['gx'=4,'gy'=4,'gz'=2] {'gy'}, use_global_device_ids=true, to_apply=%region_20.21 | all-reduce | flops 512 | bytes 4096 | tf_op jit(solution)/shard_map/psum | solution.py:193
  382.4 1.5 fusion.63
  383.9 5.7 %psum.31 = f32[2,256]{1,0:T(2,128)} all-reduce(f32[2,256]{1,0:T(2,128)S(1)} %fusion.63), channel_id=1, replica_groups=mesh['gx'=4,'gy'=4,'gz'=2] {'gz'}, use_global_device_ids=true, to_apply=%region_23.24 | all-reduce | flops 512 | bytes 4096 | tf_op jit(solution)/shard_map/psum | solution.py:199
  389.6 20.6 %reduce-scatter.9.cloned.1.call-done = bf16[3,2048,128]{1,2,0:T(8,128)(2,1)} async-done(((bf16[3,4096,128]{1,2,0:T(8,128)(2,1)}), bf16[3,2048,128]{1,2,0:T(8,128)(2,1)}) %reduce-scatter.9.cloned.1.call-update) | async-done | bytes 1572880 | tf_op jit(solution)/shard_map/reduce_scatter | solution.py:172
  410.2 3.1 copy.59
  413.2 1.0 fusion.62
  (130 shorter events, 8.0 us)
Async XLA Ops:
  7.2 2.8 copy-start
  7.2 38.2 %copy-start.12 = (s32[512]{0:T(512)S(1)}, s32[512]{0:T(512)}, u32[]{:S(2)}) copy-start(s32[512]{0:T(512)} %param.14) | copy-start | bytes 6148
  7.2 38.2 %copy-start.14 = (f32[2,256]{1,0:T(2,128)S(1)}, f32[2,256]{1,0:T(2,128)}, u32[]{:S(2)}) copy-start(f32[2,256]{1,0:T(2,128)} %param.16) | copy-start | bytes 6148
  7.2 39.2 %copy-start.4 = (bf16[128,2048]{1,0:T(8,128)(2,1)S(1)}, bf16[128,2048]{1,0:T(8,128)(2,1)}, u32[]{:S(2)}) copy-start(bf16[128,2048]{1,0:T(8,128)(2,1)} %param.18) | copy-start | bytes 1572868
  7.2 40.9 %copy-start.5 = (s32[2,8]{1,0:T(2,128)S(1)}, s32[2,8]{1,0:T(2,128)}, u32[]{:S(2)}) copy-start(s32[2,8]{1,0:T(2,128)} %param.15) | copy-start | bytes 196
  7.2 50.6 %all-gather.8.cloned.1.call-start = ((), (), s32[]{:S(2)}) async-start(), calls=%async_computation.6 | async-start | bytes 4718592 | tf_op jit(solution)/shard_map/all_gather | solution.py:35
  10.0 103.0 %all-gather.6.cloned.1.call-start = ((), (), s32[]{:S(2)}) async-start(), calls=%async_computation.5 | async-start | bytes 4456448 | tf_op jit(solution)/shard_map/all_gather | solution.py:40
  45.4 67.6 %copy-start.10 = (pred[512]{0:T(512)(128)(4,1)}, pred[512]{0:T(512)(128)(4,1)S(1)}, u32[]{:S(2)}) copy-start(pred[512]{0:T(512)(128)(4,1)S(1)} %broadcast_compare_fusion.3) | copy-start | bytes 1540
  45.4 67.6 %copy-start.8 = (f32[1,256]{1,0:T(1,128)}, f32[1,256]{1,0:T(1,128)S(1)}, u32[]{:S(2)}) copy-start(f32[1,256]{1,0:T(1,128)S(1)} %get-tuple-element.680) | copy-start | bytes 3076
  45.4 72.6 %copy-start.6 = (f32[1,256]{1,0:T(1,128)}, f32[1,256]{1,0:T(1,128)S(1)}, u32[]{:S(2)}) copy-start(f32[1,256]{1,0:T(1,128)S(1)} %get-tuple-element.679) | copy-start | bytes 3076
  46.3 97.4 %all-gather.12.cloned.1.call-start = ((), (), s32[]{:S(2)}) async-start(), calls=%async_computation.8 | async-start | bytes 1572864 | tf_op jit(solution)/shard_map/all_gather | solution.py:36
  47.4 143.9 %all-gather.14.cloned.1.call-start = ((), (), s32[]{:S(2)}) async-start(), calls=%async_computation.9 | async-start | bytes 4456448 | tf_op jit(solution)/shard_map/all_gather | solution.py:116
  48.0 171.2 %reduce-scatter.5.cloned.1.call-start = ((), (), s32[]{:S(2)}) async-start(), calls=%async_computation.10 | async-start | bytes 786432 | tf_op jit(solution)/shard_map/reduce_scatter | solution.py:152
  143.7 62.6 %copy-start.2 = (bf16[512,128]{0,1:T(8,128)(2,1)}, bf16[512,128]{0,1:T(8,128)(2,1)S(1)}, u32[]{:S(2)}) copy-start(bf16[512,128]{0,1:T(8,128)(2,1)S(1)} %copy.49) | copy-start | bytes 393220
  206.3 36.1 %reduce-scatter.11.cloned.1.call-start = ((), (), s32[]{:S(2)}) async-start(), calls=%async_computation.13 | async-start | bytes 1572864 | tf_op jit(solution)/shard_map/reduce_scatter | solution.py:175
  210.3 79.1 %all-gather.10.cloned.1.call-start = ((), (), s32[]{:S(2)}) async-start(), calls=%async_computation.7 | async-start | bytes 2228224 | tf_op jit(solution)/shard_map/all_gather | solution.py:105
  211.0 153.7 %reduce-scatter.7.cloned.1.call-start = ((), (), s32[]{:S(2)}) async-start(), calls=%async_computation.11 | async-start | bytes 4456448 | tf_op jit(solution)/shard_map/reduce_scatter | solution.py:181
  226.1 6.4 %copy-start.1 = (bf16[128,4096]{0,1:T(8,128)(2,1)S(1)}, bf16[128,4096]{0,1:T(8,128)(2,1)}, u32[]{:S(2)}) copy-start(bf16[128,4096]{0,1:T(8,128)(2,1)} %all-gather.12.cloned.1.call-done) | copy-start | bytes 3145732
  226.1 184.1 %reduce-scatter.9.cloned.1.call-start = ((), (), s32[]{:S(2)}) async-start(), calls=%async_computation.12 | async-start | bytes 4718592 | tf_op jit(solution)/shard_map/reduce_scatter | solution.py:172
  233.8 36.5 %all-to-all-start = ((bf16[128,16,256]{2,0,1:T(8,128)(2,1)}), bf16[128,16,256]{2,0,1:T(8,128)(2,1)S(1)}, u32[]{:S(2)}, u32[]{:S(2)}) async-start(bf16[128,16,256]{2,0,1:T(8,128)(2,1)} %copy.51), calls=%async_computation | async-start | bytes 2097152 | tf_op jit(solution)/shard_map/all_to_all | solution.py:106
  289.4 75.4 %copy-start.7 = (f32[1,256]{1,0:T(1,128)S(1)}, f32[1,256]{1,0:T(1,128)}, u32[]{:S(2)}) copy-start(f32[1,256]{1,0:T(1,128)} %copy-done.6) | copy-start | bytes 3076
  289.4 75.4 %copy-start.9 = (f32[1,256]{1,0:T(1,128)S(1)}, f32[1,256]{1,0:T(1,128)}, u32[]{:S(2)}) copy-start(f32[1,256]{1,0:T(1,128)} %copy-done.8) | copy-start | bytes 3076
  289.4 75.4 %copy-start.11 = (pred[512]{0:T(512)(128)(4,1)S(1)}, pred[512]{0:T(512)(128)(4,1)}, u32[]{:S(2)}) copy-start(pred[512]{0:T(512)(128)(4,1)} %copy-done.10) | copy-start | bytes 1540
  294.2 88.2 %copy-start.13 = (s32[512]{0:T(512)S(1)}, s32[512]{0:T(512)}, u32[]{:S(2)}) copy-start(s32[512]{0:T(512)} %param.14) | copy-start | bytes 6148
  364.8 48.5 %copy-start.3 = (bf16[256,512]{0,1:T(8,128)(2,1)S(1)}, bf16[256,512]{0,1:T(8,128)(2,1)}, u32[]{:S(2)}) copy-start(bf16[256,512]{0,1:T(8,128)(2,1)} %reduce-scatter.7.cloned.1.call-done) | copy-start | bytes 786436
Sparse Core Ops, SparseCore 0:
  10.1 47.6 all-gather.7
  60.5 52.4 all-gather.5
  115.1 23.5 all-gather.11
  140.6 50.6 all-gather.13
  206.4 12.7 reduce-scatter.4
  221.9 20.3 reduce-scatter.10
  245.2 44.2 all-gather.9
  293.3 71.4 reduce-scatter.6
  367.6 42.5 reduce-scatter.8
